TPU v7x, 32 devices: a whole 2x2x4 slice. The times are simulated.
32 devices in a mesh: dp: 8 (over z, y), tensor: 4 (over x, core).
Axes of the slice: x: 2, y: 2, z: 4, core: 2. Of those that a mesh axis runs over, the one named last changes fastest.
Arguments:
- tokens: bfloat16 [32768, 1024], P(('dp', 'tensor')), may hold values from -6 to 6
- segments: int32 [64, 512], P(('dp', 'tensor')), may hold values from 0 to 1, as said below
- lengths: int32 [64], P(('dp', 'tensor')), may hold values from 128 to 512, as said below
- type_table: bfloat16 [2, 1024], replicated, may hold values from -3 to 3
- attn_weight: bfloat16 [3145728], P(('dp', 'tensor')), may hold values from -0.1875 to 0.1875
- out_weight: bfloat16 [1048576], P(('dp', 'tensor')), may hold values from -0.75 to 0.75
- ffn_in_weight: bfloat16 [1024, 4096], P('dp', 'tensor'), may hold values from -0.1875 to 0.1875
- ffn_out_weight: bfloat16 [4096, 1024], P('tensor', 'dp'), may hold values from -0.125 to 0.125
- attn_bias: bfloat16 [3, 1024], replicated, may hold values from -3 to 3
- ffn_bias_in: bfloat16 [4096], replicated, may hold values from -3 to 3
- ffn_bias_out: bfloat16 [1024], replicated, may hold values from -3 to 3
- norm_gain: bfloat16 [2, 1024], replicated, may hold values from 0.099609375 to 1.8984375
- norm_shift: bfloat16 [2, 1024], replicated, may hold values from -3 to 3
- cotangent: bfloat16 [32768, 1024], P(('dp', 'tensor')), may hold values from -6 to 6
Outputs:
- output: bfloat16 [32768, 1024], P(('dp', 'tensor'))
- grad_input: bfloat16 [32768, 1024], P(('dp', 'tensor'))
- attn_bias_grad: float32 [3, 1024], replicated
- ffn_bias_in_grad: float32 [4096], replicated
- ffn_bias_out_grad: float32 [1024], replicated
- norm_gain_grad: float32 [2, 1024], replicated
- norm_shift_grad: float32 [2, 1024], replicated
Inputs may be any that keep to these rules, and one draw needn't show every extreme that they name: `lengths`: the valid tokens of a sequence are its first ones; in every draw some sequence has all 512 valid. `segments`: segment id 0 up to and including a separator at position 1 to length - 2, 1 after it up to the sequence's length, 0 on padding.
All inputs are finite; a program needn't handle non-finite values.
Results may differ from a plain program's by a relative error of at most 0.015.
Values may be sent and summed in bfloat16 or wider, within the bound.
A program may use at most 192 MiB of HBM per device.

v0:
```python
from functools import partial
import math
import jax
import jax.numpy as jnp
from jax import lax
from jax.sharding import PartitionSpec as P

HEADS = 16
HEAD = 64


def matmul(left_side, right_side):
    return jnp.dot(left_side, right_side, preferred_element_type=jnp.float32)


def matmul_t(left_side, right_side):
    return lax.dot_general(
        left_side, right_side, (((1,), (1,)), ((), ())), preferred_element_type=jnp.float32
    )


def norm_forward(residual, gain_row, shift_row):
    row_mean = jnp.mean(residual, axis=-1, keepdims=True)
    centered = residual - row_mean
    inverse = lax.rsqrt(jnp.mean(centered * centered, axis=-1, keepdims=True) + 1e-12)
    normed = centered * inverse
    return (normed * gain_row + shift_row, normed, inverse)


def norm_backward(upstream, normed, inverse, gain_row):
    scaled = upstream * gain_row
    inner = (
        scaled
        - jnp.mean(scaled, axis=-1, keepdims=True)
        - normed * jnp.mean(scaled * normed, axis=-1, keepdims=True)
    )
    return (inner * inverse, jnp.sum(upstream * normed, axis=0), jnp.sum(upstream, axis=0))


def gelu_slope(preact):
    normal_cdf = 0.5 * (1.0 + jax.scipy.special.erf(preact * 0.7071067811865476))
    normal_pdf = jnp.exp(-0.5 * preact * preact) * 0.3989422804014327
    return normal_cdf + preact * normal_pdf


def score_block(queries, key_rows, key_valid, score_scale):
    scores = (
        jnp.einsum("qhd,khd->hqk", queries, key_rows, preferred_element_type=jnp.float32)
        * score_scale
    )
    return jnp.where(key_valid[None, None, :], scores, -1000000000.0)


def context_block(block_items, score_scale):
    queries, key_rows, value_rows, key_valid = block_items
    masked = score_block(queries, key_rows, key_valid, score_scale)
    row_max = jnp.max(masked, axis=-1, keepdims=True)
    log_total = row_max + jnp.log(jnp.sum(jnp.exp(masked - row_max), axis=-1, keepdims=True))
    attn_prob = jnp.exp(masked - log_total)
    context = jnp.einsum(
        "hqk,khd->qhd",
        attn_prob.astype(jnp.bfloat16),
        value_rows,
        preferred_element_type=jnp.float32,
    )
    return (context.astype(jnp.bfloat16), log_total)


def gradient_block(block_items, score_scale):
    queries, key_rows, value_rows, key_valid, log_total, d_context = block_items
    masked = score_block(queries, key_rows, key_valid, score_scale)
    attn_prob = jnp.exp(masked - log_total)
    d_prob = jnp.einsum("qhd,khd->hqk", d_context, value_rows, preferred_element_type=jnp.float32)
    d_values = jnp.einsum(
        "hqk,qhd->khd",
        attn_prob.astype(jnp.bfloat16),
        d_context,
        preferred_element_type=jnp.float32,
    )
    row_dot = jnp.sum(d_prob * attn_prob, axis=-1, keepdims=True)
    d_scores = (attn_prob * (d_prob - row_dot)).astype(jnp.bfloat16)
    d_queries = (
        jnp.einsum("hqk,khd->qhd", d_scores, key_rows, preferred_element_type=jnp.float32)
        * score_scale
    )
    d_keys = (
        jnp.einsum("hqk,qhd->khd", d_scores, queries, preferred_element_type=jnp.float32)
        * score_scale
    )
    return (
        d_queries.astype(jnp.bfloat16),
        d_keys.astype(jnp.bfloat16),
        d_values.astype(jnp.bfloat16),
    )


def per_device(
    tokens,
    segments,
    lengths,
    type_table,
    attn_weight,
    out_weight,
    ffn_in_weight,
    ffn_out_weight,
    attn_bias,
    ffn_bias_in,
    ffn_bias_out,
    norm_gain,
    norm_shift,
    cotangent,
):
    tok_rows, model_width = tokens.shape
    seq_count, seq_len = segments.shape
    score_scale = 1.0 / math.sqrt(HEAD)
    bias_attn = attn_bias.astype(jnp.float32)
    bias_first = ffn_bias_in.astype(jnp.float32)
    bias_second = ffn_bias_out.astype(jnp.float32)
    gain_rows = norm_gain.astype(jnp.float32)
    shift_rows = norm_shift.astype(jnp.float32)
    qkv_flat, out_flat = (
        lax.all_gather(attn_weight, ("dp", "tensor"), axis=0, tiled=True),
        lax.all_gather(out_weight, ("dp", "tensor"), axis=0, tiled=True),
    )
    projections = qkv_flat.reshape(3, model_width, model_width)
    out_proj = out_flat.reshape(model_width, model_width)
    w_first, w_second = (
        lax.all_gather(ffn_in_weight, "dp", axis=0, tiled=True),
        lax.all_gather(ffn_out_weight, "dp", axis=1, tiled=True),
    )
    w_first, w_second = (
        lax.all_gather(w_first, "tensor", axis=1, tiled=True),
        lax.all_gather(w_second, "tensor", axis=0, tiled=True),
    )
    table_rows = type_table.astype(jnp.float32)
    type_rows = jnp.where(
        (segments.reshape(-1) == 1)[:, None], table_rows[1][None, :], table_rows[0][None, :]
    )
    block_input = tokens.astype(jnp.float32) + type_rows
    lowered = block_input.astype(jnp.bfloat16)
    projected = jnp.einsum("td,mde->mte", lowered, projections, preferred_element_type=jnp.float32)
    queries = (projected[0] + bias_attn[0]).astype(jnp.bfloat16)
    key_rows = projected[1].astype(jnp.bfloat16)
    value_rows = (projected[2] + bias_attn[1]).astype(jnp.bfloat16)
    head_shape = (seq_count, seq_len, HEADS, HEAD)
    query_heads = queries.reshape(head_shape)
    key_heads = key_rows.reshape(head_shape)
    value_heads = value_rows.reshape(head_shape)
    key_valid = jnp.arange(seq_len, dtype=jnp.int32)[None, :] < lengths[:, None]
    context, log_total = lax.map(
        partial(context_block, score_scale=score_scale),
        (query_heads, key_heads, value_heads, key_valid),
    )
    context = context.reshape(tok_rows, model_width)
    attn_out = matmul(context, out_proj) + bias_attn[2]
    middle, normed_one, inverse_one = norm_forward(
        block_input + attn_out, gain_rows[0], shift_rows[0]
    )
    middle_low = middle.astype(jnp.bfloat16)
    preact = matmul(middle_low, w_first) + bias_first
    hidden = jax.nn.gelu(preact, approximate=False).astype(jnp.bfloat16)
    ffn_out = matmul(hidden, w_second) + bias_second
    output_rows, normed_two, inverse_two = norm_forward(
        middle + ffn_out, gain_rows[1], shift_rows[1]
    )
    output = output_rows.astype(jnp.bfloat16)
    qkv_again, out_again = (
        lax.all_gather(attn_weight, ("dp", "tensor"), axis=0, tiled=True),
        lax.all_gather(out_weight, ("dp", "tensor"), axis=0, tiled=True),
    )
    projections = qkv_again.reshape(3, model_width, model_width)
    out_proj = out_again.reshape(model_width, model_width)
    w_first, w_second = (
        lax.all_gather(ffn_in_weight, "dp", axis=0, tiled=True),
        lax.all_gather(ffn_out_weight, "dp", axis=1, tiled=True),
    )
    w_first, w_second = (
        lax.all_gather(w_first, "tensor", axis=1, tiled=True),
        lax.all_gather(w_second, "tensor", axis=0, tiled=True),
    )
    d_second_sum, gain_two_grad, shift_two_grad = norm_backward(
        cotangent.astype(jnp.float32), normed_two, inverse_two, gain_rows[1]
    )
    d_ffn = d_second_sum.astype(jnp.bfloat16)
    bias_out_grad = jnp.sum(d_ffn.astype(jnp.float32), axis=0)
    d_preact = (matmul_t(d_ffn, w_second) * gelu_slope(preact)).astype(jnp.bfloat16)
    bias_in_grad = jnp.sum(d_preact.astype(jnp.float32), axis=0)
    d_middle_ffn = matmul_t(d_preact, w_first)
    d_middle = d_second_sum + d_middle_ffn
    d_first_sum, gain_one_grad, shift_one_grad = norm_backward(
        d_middle, normed_one, inverse_one, gain_rows[0]
    )
    d_attn = d_first_sum.astype(jnp.bfloat16)
    bias_o_grad = jnp.sum(d_attn.astype(jnp.float32), axis=0)
    d_context = matmul_t(d_attn, out_proj).astype(jnp.bfloat16).reshape(head_shape)
    d_queries, d_keys, d_values = lax.map(
        partial(gradient_block, score_scale=score_scale),
        (query_heads, key_heads, value_heads, key_valid, log_total, d_context),
    )
    d_queries = d_queries.reshape(tok_rows, model_width)
    d_keys = d_keys.reshape(tok_rows, model_width)
    d_values = d_values.reshape(tok_rows, model_width)
    bias_q_grad = jnp.sum(d_queries.astype(jnp.float32), axis=0)
    bias_v_grad = jnp.sum(d_values.astype(jnp.float32), axis=0)
    stacked = jnp.stack([d_queries, d_keys, d_values])
    d_input = d_first_sum + jnp.einsum(
        "mte,mde->td", stacked, projections, preferred_element_type=jnp.float32
    )
    grad_input = d_input.astype(jnp.bfloat16)
    attn_grad = jnp.stack([bias_q_grad, bias_v_grad, bias_o_grad])
    gain_grad = jnp.stack([gain_one_grad, gain_two_grad])
    shift_grad = jnp.stack([shift_one_grad, shift_two_grad])
    attn_grad, bias_in_grad, bias_out_grad, gain_grad, shift_grad = lax.psum(
        (attn_grad, bias_in_grad, bias_out_grad, gain_grad, shift_grad), ("dp", "tensor")
    )
    return (output, grad_input, attn_grad, bias_in_grad, bias_out_grad, gain_grad, shift_grad)


def solution(mesh):
    in_specs = (
        P(("dp", "tensor"), None),
        P(("dp", "tensor"), None),
        P(("dp", "tensor")),
        P(),
        P(("dp", "tensor")),
        P(("dp", "tensor")),
        P("dp", "tensor"),
        P("tensor", "dp"),
        P(),
        P(),
        P(),
        P(),
        P(),
        P(("dp", "tensor"), None),
    )
    out_specs = (P(("dp", "tensor"), None), P(("dp", "tensor"), None), P(), P(), P(), P(), P())
    return jax.shard_map(
        per_device, mesh=mesh, in_specs=in_specs, out_specs=out_specs, check_vma=False
    )
```

profile of v0, /device:TPU:0, one launch (start us, length us, event | category | flops | bytes accessed | tf_op | source)
XLA Modules:
  0.0 693.1 jit_solution(5041062795089590468)
XLA Ops:
  10.0 51.9 %all-gather.11.cloned.1.call-done = bf16[1024,1024]{1,0:T(8,128)(2,1)} async-done(((bf16[128,1024]{1,0:T(8,128)(2,1)}), bf16[1024,1024]{1,0:T(8,128)(2,1)}) %all-gather.11.cloned.1.call-update) | async-done | bytes 2097168 | tf_op jit(solution)/shard_map/all_gather | solution.py:128
  67.5 3.9 copy.85
  72.7 40.2 %all-gather.15.cloned.1.call-done = bf16[1024,1024]{1,0:T(8,128)(2,1)} async-done(((bf16[1024,128]{1,0:T(8,128)(2,1)}), bf16[1024,1024]{1,0:T(8,128)(2,1)}) %all-gather.15.cloned.1.call-update) | async-done | bytes 2097168 | tf_op jit(solution)/shard_map/all_gather | solution.py:129
  113.0 57.3 %all-gather.9.cloned.1.call-done = bf16[1048576]{0:T(1024)(128)(2,1)} async-done(((bf16[32768]{0:T(1024)(128)(2,1)}), bf16[1048576]{0:T(1024)(128)(2,1)}) %all-gather.9.cloned.1.call-update) | async-done | bytes 2097168 | tf_op jit(solution)/shard_map/all_gather | solution.py:123
  170.2 4.1 reshape.135
  174.4 66.6 %all-gather.7.cloned.1.call-done = bf16[3145728]{0:T(1024)(128)(2,1)} async-done(((bf16[98304]{0:T(1024)(128)(2,1)}), bf16[3145728]{0:T(1024)(128)(2,1)}) %all-gather.7.cloned.1.call-update) | async-done | bytes 6291472 | tf_op jit(solution)/shard_map/all_gather | solution.py:122
  241.0 10.6 %reshape.133 = bf16[3,1024,1024]{2,1,0:T(8,128)(2,1)} reshape(bf16[3145728]{0:T(1024)(128)(2,1)} %all-gather.7.cloned.1.call-done) | data formatting | bytes 12582912 | tf_op jit(solution)/shard_map/reshape | solution.py:125
  251.5 11.7 %convolution_bitcast_fusion = f32[3,1024,1024]{2,1,0:T(8,128)S(1)} fusion(bf16[3,1024,1024]{2,1,0:T(8,128)(2,1)} %reshape.133, bf16[1024,1024]{0,1:T(8,128)(2,1)S(1)} %copy-done.22, f32[1024]{0:T(1024)S(1)} %bitcast.169, f32[1024]{0:T(1024)S(1)} %bitcast.167, pred[1024]{0:T(1024)(128)(4,1)S(1)} %eq.15), kind=kOutput, calls=%fused_computation.99 | convolution fusion | flops 6446645248 | bytes 20980736 | tf_op jit(solution)/shard_map/td,mde->mte/dot_general | solution.py:141
  263.5 4.1 fusion.135
  267.7 5.4 copy.77
  273.1 6.6 squeeze.34
  279.7 3.9 add_convert_fusion.2
  285.4 5.4 copy.78
  290.8 6.6 squeeze.35
  297.4 3.9 add_convert_fusion.1
  303.2 4.0 reshape.143
  307.2 4.9 copy.82
  313.7 28.0 %while.26 = (s32[]{:T(128)}, bf16[2,512,16,64]{1,3,2,0:T(8,128)(2,1)}, f32[2,16,512,1]{2,1,3,0:T(8,128)S(1)}, bf16[2,512,16,64]{1,3,2,0:T(8,128)(2,1)}, pred[2,5...) while((s32[]{:T(128)}, ...), condition=%wide.region_3.4_spmd, body=%wide.region_0.3_spmd.sunk | while | flops 1120395264 | bytes 63181432 | solution.py:150
  313.7 5.1 fusion.169
  322.7 4.8 fusion.170
  327.5 5.0 fusion.169
  336.4 4.8 fusion.170
  341.7 4.6 copy.83
  352.3 16.8 %fusion.90 = f32[1024,4096]{1,0:T(8,128)} fusion(bf16[1024,4096]{1,0:T(8,128)(2,1)} %all-gather.13.cloned.1.call-done, f32[1024,1024]{0,1:T(8,128)} %copy-done.11, f32[1024]{0:T(1024)S(1)} %bitcast.165, f32[1024]{0:T(1024)S(1)} %bitcast.156, f32[1024]{0:T(1024)S(1)} %add_rsqrt_fusion.1, f32[1024]{0:T(1024)S(1)} %broadcast_multiply_fusion.5), kind=kOutput, calls=%fused_computation.128 | convolution fusion | flops 8595177472 | bytes 29376512 | tf_op jit(solution)/shard_map/dot_general | solution.py:13
  369.2 51.3 %fusion.140 = (f32[1024]{0:T(1024)S(1)}, f32[1024,1024]{0,1:T(8,128)}) fusion(f32[1024]{0:T(1024)S(1)} %copy-done.47, bf16[4096,1024]{1,0:T(8,128)(2,1)} %all-gather.17.cloned.1.call-done, f32[1024,4096]{1,0:T(8,128)} %fusion.90, f32[4096]{0:T(1024)S(1)} %copy-done.40, f32[1024]{0:T(1024)S(1)} %bitcast.166, f32[1024]{0:T(1024)S(1)} %bitcast.157, ...), kind=kOutput, calls=%fused_computation.192 | convolution fusion | flops 8874097664 | bytes 33595392 | tf_op jit(solution)/shard_map/dot_general | solution.py:13
  425.0 22.0 %convert_reduce_fusion = (f32[4096]{0:T(1024)}, bf16[1024,4096]{1,0:T(8,128)(2,1)}) fusion(f32[1024,4096]{1,0:T(8,128)} %fusion.90, f32[4096]{0:T(1024)S(1)} %copy-done.40, bf16[4096,1024]{1,0:T(8,128)(2,1)} %all-gather.17.cloned.1.call-done, f32[1024]{0:T(1024)S(1)} %get-tuple-element.250, f32[1024]{0:T(1024)S(1)} %add_rsqrt_fusion, ...), kind=kOutput, calls=%fused_computation.70 | convolution fusion | flops 8653893632 | bytes 39899136 | tf_op jit(solution)/shard_map/dot_general | solution.py:17
  447.1 17.5 %multiply_reduce_fusion.1 = (f32[1024]{0:T(1024)}, f32[1024]{0:T(1024)S(1)}, f32[1024]{0:T(1024)S(1)}, f32[1024]{0:T(1024)}, f32[1024,1024]{0,1:T(8,128)S(1)}) fusion(f32[1024,1024]{0,1:T(8,128)} %copy-done.11, f32[1024]{0:T(1024)S(1)} %add_rsqrt_fusion.1, f32[1024]{0:T(1024)S(1)} %broadcast_multiply_fusion.5, f32[1024]{0:T(1024)S(1)} %bitcast.158, ...), kind=kOutput, calls=%fused_computation.107 | convolution fusion | flops 8608804864 | bytes 31506432 | tf_op jit(solution)/shard_map/dot_general | solution.py:17
  471.1 4.0 reshape.139
  475.1 5.4 copy.90
  485.2 93.9 %while.27 = (s32[]{:T(128)}, bf16[2,512,16,64]{1,3,2,0:T(8,128)(2,1)}, bf16[2,512,16,64]{1,3,2,0:T(8,128)(2,1)}, bf16[2,512,16,64]{1,3,2,0:T(8,128)(2,1)}, bf16[...) while((s32[]{:T(128)}, ...), condition=%wide.region_14.15_spmd, body=%wide.region_12.14_spmd.sunk | while | flops 2724716544 | bytes 195205968 | solution.py:196
  485.3 9.6 %subtract_exponential_fusion.2 = f32[16,512,512]{1,2,0:T(8,128)} fusion(f32[16,512]{1,0:T(8,128)S(1)} %dynamic-slice_bitcast_fusion.2, pred[512]{0:T(512)(128)(4,1)S(1)} %dynamic-slice_reduce_fusion.5, bf16[2,512,16,64]{1,3,2,0:T(8,128)(2,1)} %get-tuple-element.420, s32[]{:T(128)} %get-tuple-element.403, ...), kind=kOutput, calls=%fused_computation.25.clone.1 | convolution fusion | flops 549453824 | bytes 18908672 | tf_op jit(solution)/shard_map/while/body/eval_jaxpr/qhd,khd->hqk/dot_general | solution.py:48
  494.9 10.5 %multiply_reduce_fusion.7 = (f32[16,512]{1,0:T(8,128)S(1)}, f32[16,512,512]{1,2,0:T(8,128)}) fusion(f32[16,512,512]{1,2,0:T(8,128)} %subtract_exponential_fusion.2, bf16[2,512,16,64]{1,3,2,0:T(8,128)(2,1)S(1)} %copy-done.6, s32[]{:T(128)} %get-tuple-element.403, bf16[2,512,16,64]{1,3,2,0:T(8,128)(2,1)S(1)} %copy-done.2), kind=kOutput, calls=%fused_computation.24.clone.1 | convolution fusion | flops 545251328 | bytes 35685376 | tf_op jit(solution)/shard_map/while/body/eval_jaxpr/qhd,khd->hqk/dot_general | solution.py:73
  505.4 11.9 %multiply_convert_fusion.4 = bf16[16,512,512]{1,2,0:T(8,128)(2,1)S(1)} fusion(f32[16,512,512]{1,2,0:T(8,128)} %subtract_exponential_fusion.2, f32[16,512,512]{1,2,0:T(8,128)} %get-tuple-element.366, f32[16,512]{1,0:T(8,128)S(1)} %get-tuple-element.367), kind=kLoop, calls=%fused_computation.23.clone.1 | loop fusion | flops 12582912 | bytes 41975808 | tf_op jit(solution)/shard_map/while/body/eval_jaxpr/convert_element_type | solution.py:81
  522.8 9.4 %fusion.181 = bf16[2,512,16,64]{1,3,2,0:T(8,128)(2,1)} fusion(bf16[2,512,16,64]{1,3,2,0:T(8,128)(2,1)} %get-tuple-element.406, s32[]{:T(128)} %get-tuple-element.403, f32[16,512,512]{1,2,0:T(8,128)} %subtract_exponential_fusion.2, bf16[2,512,16,64]{1,3,2,0:T(8,128)(2,1)S(1)} %copy-done.2), kind=kOutput, calls=%fused_computation.36.clone.1 | convolution fusion | flops 541589504 | bytes 18875392 | tf_op jit(solution)/shard_map/while/body/eval_jaxpr/hqk,qhd->khd/dot_general | solution.py:74
  532.2 9.6 %subtract_exponential_fusion.2 = f32[16,512,512]{1,2,0:T(8,128)} fusion(f32[16,512]{1,0:T(8,128)S(1)} %dynamic-slice_bitcast_fusion.2, pred[512]{0:T(512)(128)(4,1)S(1)} %dynamic-slice_reduce_fusion.5, bf16[2,512,16,64]{1,3,2,0:T(8,128)(2,1)} %get-tuple-element.420, s32[]{:T(128)} %get-tuple-element.403, ...), kind=kOutput, calls=%fused_computation.25.clone.1 | convolution fusion | flops 549453824 | bytes 18908672 | tf_op jit(solution)/shard_map/while/body/eval_jaxpr/qhd,khd->hqk/dot_general | solution.py:48
  541.9 10.5 %multiply_reduce_fusion.7 = (f32[16,512]{1,0:T(8,128)S(1)}, f32[16,512,512]{1,2,0:T(8,128)}) fusion(f32[16,512,512]{1,2,0:T(8,128)} %subtract_exponential_fusion.2, bf16[2,512,16,64]{1,3,2,0:T(8,128)(2,1)S(1)} %copy-done.6, s32[]{:T(128)} %get-tuple-element.403, bf16[2,512,16,64]{1,3,2,0:T(8,128)(2,1)S(1)} %copy-done.2), kind=kOutput, calls=%fused_computation.24.clone.1 | convolution fusion | flops 545251328 | bytes 35685376 | tf_op jit(solution)/shard_map/while/body/eval_jaxpr/qhd,khd->hqk/dot_general | solution.py:73
  552.3 11.9 %multiply_convert_fusion.4 = bf16[16,512,512]{1,2,0:T(8,128)(2,1)S(1)} fusion(f32[16,512,512]{1,2,0:T(8,128)} %subtract_exponential_fusion.2, f32[16,512,512]{1,2,0:T(8,128)} %get-tuple-element.366, f32[16,512]{1,0:T(8,128)S(1)} %get-tuple-element.367), kind=kLoop, calls=%fused_computation.23.clone.1 | loop fusion | flops 12582912 | bytes 41975808 | tf_op jit(solution)/shard_map/while/body/eval_jaxpr/convert_element_type | solution.py:81
  569.7 9.4 %fusion.181 = bf16[2,512,16,64]{1,3,2,0:T(8,128)(2,1)} fusion(bf16[2,512,16,64]{1,3,2,0:T(8,128)(2,1)} %get-tuple-element.406, s32[]{:T(128)} %get-tuple-element.403, f32[16,512,512]{1,2,0:T(8,128)} %subtract_exponential_fusion.2, bf16[2,512,16,64]{1,3,2,0:T(8,128)(2,1)S(1)} %copy-done.2), kind=kOutput, calls=%fused_computation.36.clone.1 | convolution fusion | flops 541589504 | bytes 18875392 | tf_op jit(solution)/shard_map/while/body/eval_jaxpr/hqk,qhd->khd/dot_general | solution.py:74
  581.1 6.2 copy.112
  589.4 6.2 copy.114
  595.6 5.5 fusion.82
  601.3 6.6 reshape.140
  607.9 4.8 copy.113
  612.6 6.5 reshape.141
  619.2 6.6 reshape.142
  625.8 12.7 %fusion.83 = bf16[1024,1024]{0,1:T(8,128)(2,1)} fusion(f32[1024,1024]{0,1:T(8,128)} %copy-done.17, bf16[3,1024,1024]{2,1,0:T(8,128)(2,1)} %reshape.133, bf16[1,1024,1024]{2,1,0:T(8,128)(2,1)} %reshape.142, bf16[1,1024,1024]{2,1,0:T(8,128)(2,1)} %reshape.141, bf16[1,1024,1024]{2,1,0:T(8,128)(2,1)S(1)} %copy-done.18), kind=kOutput, calls=%fused_computation.106 | convolution fusion | flops 6450839552 | bytes 18874368 | tf_op jit(solution)/shard_map/mte,mde->td/dot_general | solution.py:206
  638.5 4.1 copy.100
  645.2 40.6 %all-reduce = (f32[3,1024]{1,0:T(4,128)}, f32[4096]{0:T(1024)}, f32[1024]{0:T(1024)}, f32[2,1024]{1,0:T(2,128)}, f32[2,1024]{1,0:T(2,128)}) all-reduce(f32[3,1024]{1,0:T(4,128)S(1)} %pad_maximum_fusion, f32[4096]{0:T(1024)S(1)} %copy-done.41, f32[1024]{0:T(1024)S(1)} %get-tuple-element.179, ...), channel_id=1, replica_groups=mesh['dp'=8,'tensor'=4] {'dp','tensor'}, use_global_device_ids=true, to_apply=%region_18.19 | all-reduce | flops 12288 | bytes 98304 | tf_op jit(solution)/shard_map/psum | solution.py:213
  (192 shorter events, 62.2 us)
Async XLA Ops:
  7.2 56.3 %copy-start.19 = (bf16[1024,1024]{1,0:T(8,128)(2,1)S(1)}, bf16[1024,1024]{1,0:T(8,128)(2,1)}, u32[]{:S(2)}) copy-start(bf16[1024,1024]{1,0:T(8,128)(2,1)} %param.18) | copy-start | bytes 6291460
  7.2 58.9 %copy-start.46 = (s32[2,512]{1,0:T(2,128)S(1)}, s32[2,512]{1,0:T(2,128)}, u32[]{:S(2)}) copy-start(s32[2,512]{1,0:T(2,128)} %param.19) | copy-start | bytes 12292
  7.2 59.1 %copy-start.45 = (bf16[4096]{0:T(1024)(128)(2,1)S(1)}, bf16[4096]{0:T(1024)(128)(2,1)}, u32[]{:S(2)}) copy-start(bf16[4096]{0:T(1024)(128)(2,1)} %param.27) | copy-start | bytes 24580
  7.2 59.7 %copy-start.50 = (bf16[1024]{0:T(1024)(128)(2,1)S(1)}, bf16[1024]{0:T(1024)(128)(2,1)}, u32[]{:S(2)}) copy-start(bf16[1024]{0:T(1024)(128)(2,1)} %param.28) | copy-start | bytes 6148
  7.2 54.8 %all-gather.11.cloned.1.call-start = ((), (), s32[]{:S(2)}) async-start(), calls=%async_computation.2 | async-start | bytes 2359296 | tf_op jit(solution)/shard_map/all_gather | solution.py:128
  7.9 105.0 %all-gather.15.cloned.1.call-start = ((), (), s32[]{:S(2)}) async-start(), calls=%async_computation.4 | async-start | bytes 2359296 | tf_op jit(solution)/shard_map/all_gather | solution.py:129
  8.7 161.5 %all-gather.9.cloned.1.call-start = ((), (), s32[]{:S(2)}) async-start(), calls=%async_computation.1 | async-start | bytes 2162688 | tf_op jit(solution)/shard_map/all_gather | solution.py:123
  9.4 231.6 %all-gather.7.cloned.1.call-start = ((), (), s32[]{:S(2)}) async-start(), calls=%async_computation | async-start | bytes 6488064 | tf_op jit(solution)/shard_map/all_gather | solution.py:122
  10.0 342.3 %all-gather.13.cloned.1.call-start = ((), (), s32[]{:S(2)}) async-start(), calls=%async_computation.3 | async-start | bytes 10485760 | tf_op jit(solution)/shard_map/all_gather | solution.py:132
  62.0 307.2 %all-gather.17.cloned.1.call-start = ((), (), s32[]{:S(2)}) async-start(), calls=%async_computation.5 | async-start | bytes 10485760 | tf_op jit(solution)/shard_map/all_gather | solution.py:133
  63.5 8.0 %copy-start.51 = (s32[2]{0:T(128)S(1)}, s32[2]{0:T(128)}, u32[]{:S(2)}) copy-start(s32[2]{0:T(128)} %param.20) | copy-start | bytes 28
  63.5 8.0 %copy-start.42 = (bf16[2,1024]{1,0:T(2,128)(2,1)S(1)}, bf16[2,1024]{1,0:T(2,128)(2,1)}, u32[]{:S(2)}) copy-start(bf16[2,1024]{1,0:T(2,128)(2,1)} %param.21) | copy-start | bytes 12292
  63.5 8.0 %copy-start.43 = (bf16[2,1024]{1,0:T(2,128)(2,1)S(1)}, bf16[2,1024]{1,0:T(2,128)(2,1)}, u32[]{:S(2)}) copy-start(bf16[2,1024]{1,0:T(2,128)(2,1)} %param.29) | copy-start | bytes 12292
  63.5 8.6 %copy-start.44 = (bf16[2,1024]{1,0:T(2,128)(2,1)S(1)}, bf16[2,1024]{1,0:T(2,128)(2,1)}, u32[]{:S(2)}) copy-start(bf16[2,1024]{1,0:T(2,128)(2,1)} %param.30) | copy-start | bytes 12292
  174.4 77.2 %copy-start.22 = (bf16[1024,1024]{0,1:T(8,128)(2,1)S(1)}, bf16[1024,1024]{0,1:T(8,128)(2,1)}, u32[]{:S(2)}) copy-start(bf16[1024,1024]{0,1:T(8,128)(2,1)} %copy.75) | copy-start | bytes 6291460
  341.7 5.2 copy-start
  341.7 5.2 copy-start.24
  341.7 5.2 copy-start.26
  341.7 5.2 copy-start.20
  352.3 16.9 %copy-start.40 = (f32[4096]{0:T(1024)S(1)}, f32[4096]{0:T(1024)}, u32[]{:S(2)}) copy-start(f32[4096]{0:T(1024)} %convert_element_type.124) | copy-start | bytes 49156
  352.3 16.9 %copy-start.47 = (f32[1024]{0:T(1024)S(1)}, f32[1024]{0:T(1024)}, u32[]{:S(2)}) copy-start(f32[1024]{0:T(1024)} %convert_element_type.126) | copy-start | bytes 12292
  369.2 54.2 %copy-start.9 = (bf16[1024,1024]{0,1:T(8,128)(2,1)S(1)}, bf16[1024,1024]{0,1:T(8,128)(2,1)}, u32[]{:S(2)}) copy-start(bf16[1024,1024]{0,1:T(8,128)(2,1)} %copy.85) | copy-start | bytes 6291460
  420.6 26.5 %copy-start.28 = (f32[1024]{0:T(1024)}, f32[1024]{0:T(1024)S(1)}, u32[]{:S(2)}) copy-start(f32[1024]{0:T(1024)S(1)} %broadcast_multiply_fusion.4) | copy-start | bytes 12292
  423.4 23.7 %copy-start.30 = (f32[1024]{0:T(1024)}, f32[1024]{0:T(1024)S(1)}, u32[]{:S(2)}) copy-start(f32[1024]{0:T(1024)S(1)} %add_rsqrt_fusion) | copy-start | bytes 12292
  425.0 22.1 %copy-start.36 = (f32[1024]{0:T(1024)}, f32[1024]{0:T(1024)S(1)}, u32[]{:S(2)}) copy-start(f32[1024]{0:T(1024)S(1)} %get-tuple-element.250) | copy-start | bytes 12292
  425.0 22.1 %copy-start.38 = (f32[1024]{0:T(1024)}, f32[1024]{0:T(1024)S(1)}, u32[]{:S(2)}) copy-start(f32[1024]{0:T(1024)S(1)} %get-tuple-element.251) | copy-start | bytes 12292
  447.1 17.5 %copy-start.12 = (f32[1024,1024]{0,1:T(8,128)S(1)}, f32[1024,1024]{0,1:T(8,128)}, u32[]{:S(2)}) copy-start(f32[1024,1024]{0,1:T(8,128)} %copy-done.11) | copy-start | bytes 12582916
  485.3 9.7 %copy-start.2 = (bf16[2,512,16,64]{1,3,2,0:T(8,128)(2,1)S(1)}, bf16[2,512,16,64]{1,3,2,0:T(8,128)(2,1)}, u32[]{:S(2)}) copy-start(bf16[2,512,16,64]{1,3,2,0:T(8,128)(2,1)} %get-tuple-element.422) | copy-start | bytes 6291460 | tf_op jit(solution)/shard_map/while
  485.3 9.6 %copy-start.6 = (bf16[2,512,16,64]{1,3,2,0:T(8,128)(2,1)S(1)}, bf16[2,512,16,64]{1,3,2,0:T(8,128)(2,1)}, u32[]{:S(2)}) copy-start(bf16[2,512,16,64]{1,3,2,0:T(8,128)(2,1)} %get-tuple-element.423) | copy-start | bytes 6291460 | tf_op jit(solution)/shard_map/while
  505.4 11.9 %copy-start.3 = (bf16[2,512,16,64]{1,3,2,0:T(8,128)(2,1)S(1)}, bf16[2,512,16,64]{1,3,2,0:T(8,128)(2,1)}, u32[]{:S(2)}) copy-start(bf16[2,512,16,64]{1,3,2,0:T(8,128)(2,1)} %get-tuple-element.420) | copy-start | bytes 6291460 | tf_op jit(solution)/shard_map/while
  505.4 11.9 %copy-start.13 = (bf16[2,512,16,64]{1,3,2,0:T(8,128)(2,1)S(1)}, bf16[2,512,16,64]{1,3,2,0:T(8,128)(2,1)}, u32[]{:S(2)}) copy-start(bf16[2,512,16,64]{1,3,2,0:T(8,128)(2,1)} %get-tuple-element.405) | copy-start | bytes 6291460 | tf_op jit(solution)/shard_map/while
  532.2 9.6 %copy-start.2 = (bf16[2,512,16,64]{1,3,2,0:T(8,128)(2,1)S(1)}, bf16[2,512,16,64]{1,3,2,0:T(8,128)(2,1)}, u32[]{:S(2)}) copy-start(bf16[2,512,16,64]{1,3,2,0:T(8,128)(2,1)} %get-tuple-element.422) | copy-start | bytes 6291460 | tf_op jit(solution)/shard_map/while
  532.2 9.6 %copy-start.6 = (bf16[2,512,16,64]{1,3,2,0:T(8,128)(2,1)S(1)}, bf16[2,512,16,64]{1,3,2,0:T(8,128)(2,1)}, u32[]{:S(2)}) copy-start(bf16[2,512,16,64]{1,3,2,0:T(8,128)(2,1)} %get-tuple-element.423) | copy-start | bytes 6291460 | tf_op jit(solution)/shard_map/while
  552.3 11.9 %copy-start.3 = (bf16[2,512,16,64]{1,3,2,0:T(8,128)(2,1)S(1)}, bf16[2,512,16,64]{1,3,2,0:T(8,128)(2,1)}, u32[]{:S(2)}) copy-start(bf16[2,512,16,64]{1,3,2,0:T(8,128)(2,1)} %get-tuple-element.420) | copy-start | bytes 6291460 | tf_op jit(solution)/shard_map/while
  552.3 11.9 %copy-start.13 = (bf16[2,512,16,64]{1,3,2,0:T(8,128)(2,1)S(1)}, bf16[2,512,16,64]{1,3,2,0:T(8,128)(2,1)}, u32[]{:S(2)}) copy-start(bf16[2,512,16,64]{1,3,2,0:T(8,128)(2,1)} %get-tuple-element.405) | copy-start | bytes 6291460 | tf_op jit(solution)/shard_map/while
  587.2 8.3 %copy-start.10 = (bf16[1024,1024]{0,1:T(8,128)(2,1)S(1)}, bf16[1024,1024]{0,1:T(8,128)(2,1)}, u32[]{:S(2)}) copy-start(bf16[1024,1024]{0,1:T(8,128)(2,1)} %copy.85) | copy-start | bytes 6291460
  587.2 8.3 %copy-start.29 = (f32[1024]{0:T(1024)S(1)}, f32[1024]{0:T(1024)}, u32[]{:S(2)}) copy-start(f32[1024]{0:T(1024)} %copy-done.28) | copy-start | bytes 12292
  587.3 8.3 %copy-start.31 = (f32[1024]{0:T(1024)S(1)}, f32[1024]{0:T(1024)}, u32[]{:S(2)}) copy-start(f32[1024]{0:T(1024)} %copy-done.30) | copy-start | bytes 12292
  587.3 8.3 %copy-start.33 = (f32[1,1024]{1,0:T(1,128)S(1)}, f32[1,1024]{1,0:T(1,128)}, u32[]{:S(2)}) copy-start(f32[1,1024]{1,0:T(1,128)} %get-tuple-element.237) | copy-start | bytes 12292
  587.3 8.4 %copy-start.35 = (f32[1,1024]{1,0:T(1,128)S(1)}, f32[1,1024]{1,0:T(1,128)}, u32[]{:S(2)}) copy-start(f32[1,1024]{1,0:T(1,128)} %get-tuple-element.239) | copy-start | bytes 12292
  587.3 8.3 %copy-start.37 = (f32[1024]{0:T(1024)S(1)}, f32[1024]{0:T(1024)}, u32[]{:S(2)}) copy-start(f32[1024]{0:T(1024)} %copy-done.36) | copy-start | bytes 12292
  587.3 8.3 %copy-start.39 = (f32[1024]{0:T(1024)S(1)}, f32[1024]{0:T(1024)}, u32[]{:S(2)}) copy-start(f32[1024]{0:T(1024)} %copy-done.38) | copy-start | bytes 12292
  601.1 6.8 copy-start.15
  619.2 6.6 copy-start.18
  638.5 6.7 copy-start.49
  638.5 6.7 copy-start.48
  638.5 6.7 copy-start.34
  638.5 6.7 copy-start.41
  (18 other events, 57.0 us)
Sparse Core Ops, SparseCore 0:
  10.1 51.7 all-gather.10
  64.0 48.8 all-gather.14
  115.8 54.3 all-gather.8
  172.9 67.9 all-gather.6
  242.4 56.7 all-gather.12
  300.6 58.2 all-gather.16
where the time goes:
time: 704 us; the launch traced here: 693 us
  matrix products  224 us (32%)
  waiting for transfers between devices  219 us (31%)
  local copies, waits for them, and re-layouts  136 us (19%)
  other arithmetic  57.2 us (8%)
  blocking collectives  40.6 us (6%)
  between operations  15.1 us (2%)
    dot_general x3, matrix products, matmul(): return jnp.dot(left_side, right_side, preferred_element_type=jnp.float32)  71.1 us
    all_gather x1, waiting for transfers between devices, per_device(): lax.all_gather(attn_weight, ('dp', 'tensor'), axis=0, tiled=True)  66.6 us
    all_gather x1, waiting for transfers between devices, per_device(): lax.all_gather(out_weight, ('dp', 'tensor'), axis=0, tiled=True)  57.3 us
    all_gather x1, waiting for transfers between devices, per_device(): lax.all_gather(ffn_in_weight, 'dp', axis=0, tiled=True)  51.9 us
    dot_general x3, matrix products, matmul_t(): lax.dot_general(left_side, right_side, (((1,), (1,)), ((), ())), preferre...  42 us
    psum x1, blocking collectives, per_device(): lax.psum((attn_grad, bias_in_grad, bias_out_grad, gain_grad, shift_grad),...  40.6 us
    all_gather x1, waiting for transfers between devices, per_device(): lax.all_gather(ffn_out_weight, 'dp', axis=1, tiled=True)  40.2 us
    another operation x6, local copies, waits for them, and re-layouts, per_device(): stacked = jnp.stack([d_queries, d_keys, d_values])  36.9 us
  transfers between devices with their start and end apart: 6, of which 4 were waited for; matrix products, arithmetic and copies ran while one was open for 20% of the time, Pallas kernels for 0%

commit v1 on v0

--- a/solution.py
+++ b/solution.py
@@ -7,6 +7,28 @@
 
 HEADS = 16
 HEAD = 64
+
+
+def joined_along(parts, dim):
+    shape = list(parts.shape[1:])
+    shape[dim] *= parts.shape[0]
+    return jnp.moveaxis(parts, 0, dim).reshape(shape)
+
+
+def collect(x, axis, dim):
+    count = lax.axis_size(axis)
+    pairs = [(i, (i + 1) % count) for i in range(count)]
+    back = [(b, a) for a, b in pairs]
+    lower, upper = ([], [])
+    for step in range(count - 1):
+        if step % 2 == 0:
+            lower.append(lax.ppermute(lower[-1] if lower else x, axis, pairs))
+        else:
+            upper.append(lax.ppermute(upper[-1] if upper else x, axis, back))
+    blocks = jnp.stack([*lower[::-1], x, *upper])
+    shift = lax.axis_index(axis) - len(lower)
+    blocks = blocks[(jnp.arange(count) - shift) % count]
+    return joined_along(blocks, dim)
 
 
 def matmul(left_side, right_side):
@@ -125,7 +147,7 @@
     projections = qkv_flat.reshape(3, model_width, model_width)
     out_proj = out_flat.reshape(model_width, model_width)
     w_first, w_second = (
-        lax.all_gather(ffn_in_weight, "dp", axis=0, tiled=True),
+        collect(ffn_in_weight, "dp", 0),
         lax.all_gather(ffn_out_weight, "dp", axis=1, tiled=True),
     )
     w_first, w_second = (

time: 704 us -> 728 us (1.034)
  starting transfers between devices: 0.23 us -> 15.2 us
    ppermute x0 -> x7, waiting for transfers between devices: none -> 42 us  [the longest x4 39.5 us: collect(): lower.append(lax.ppermute(lower[-1] if lower else x, axis, pairs))]
    all_gather x1, waiting for transfers between devices: 40.2 us -> 10.4 us  [per_device(): lax.all_gather(ffn_out_weight, 'dp', axis=1, tiled=True)]
    ppermute x0 -> x7, starting transfers between devices: none -> 15 us  [the longest x3 8.03 us: collect(): upper.append(lax.ppermute(upper[-1] if upper else x, axis, back))]
    all_gather x1, waiting for transfers between devices: 51.9 us -> 41.6 us  [per_device(): lax.all_gather(ffn_in_weight, 'dp', axis=0, tiled=True)]
    unnamed x93 -> x102, local copies, waits for them, and re-layouts: 18.4 us -> 20.6 us
  transfers between devices with their start and end apart: 6 -> 14, of which waited for: 4 -> 9; matrix products, arithmetic and copies ran while one was open for 20% -> 31% of each run, Pallas kernels for 0% -> 0%
where the time goes in v1:
time: 728 us; the launch traced here: 717 us
  matrix products  228 us (31%)
  waiting for transfers between devices  221 us (30%)
  local copies, waits for them, and re-layouts  140 us (19%)
  other arithmetic  56.5 us (8%)
  blocking collectives  40.5 us (6%)
  starting transfers between devices  15.2 us (2%)
  between operations  15.2 us (2%)
    dot_general x3, matrix products, matmul(): return jnp.dot(left_side, right_side, preferred_element_type=jnp.float32)  73.2 us
    all_gather x1, waiting for transfers between devices, per_device(): lax.all_gather(attn_weight, ('dp', 'tensor'), axis=0, tiled=True)  66.6 us
    all_gather x1, waiting for transfers between devices, per_device(): lax.all_gather(out_weight, ('dp', 'tensor'), axis=0, tiled=True)  57.6 us
    dot_general x3, matrix products, matmul_t(): lax.dot_general(left_side, right_side, (((1,), (1,)), ((), ())), preferre...  43 us
    all_gather x1, waiting for transfers between devices, per_device(): lax.all_gather(ffn_in_weight, 'dp', axis=0, tiled=True)  41.6 us
    psum x1, blocking collectives, per_device(): lax.psum((attn_grad, bias_in_grad, bias_out_grad, gain_grad, shift_grad),...  40.5 us
    ppermute x4, waiting for transfers between devices, collect(): lower.append(lax.ppermute(lower[-1] if lower else x, axis, pairs))  39.5 us
    another operation x6, local copies, waits for them, and re-layouts, per_device(): stacked = jnp.stack([d_queries, d_keys, d_values])  36.9 us
  transfers between devices with their start and end apart: 14, of which 9 were waited for; matrix products, arithmetic and copies ran while one was open for 31% of the time, Pallas kernels for 0%

profile of v1, /device:TPU:0, one launch (start us, length us, event | category | flops | bytes accessed | tf_op | source)
XLA Modules:
  0.0 716.9 jit_solution(17740626177619197799)
XLA Ops:
  13.1 9.6 %collective-permute-done = bf16[128,1024]{1,0:T(8,128)(2,1)S(1)} collective-permute-done((bf16[128,1024]{1,0:T(8,128)(2,1)}, bf16[128,1024]{1,0:T(8,128)(2,1)S(1)}, u32[]{:S(2)}, u32[]{:S(2)}) %collective-permute-start) | collective-permute-done | bytes 262176 | tf_op jit(solution)/shard_map/ppermute | solution.py:25
  22.6 4.7 collective-permute-start.4
  27.3 9.0 %collective-permute-done.1 = bf16[128,1024]{1,0:T(8,128)(2,1)S(1)} collective-permute-done((bf16[128,1024]{1,0:T(8,128)(2,1)S(1)}, bf16[128,1024]{1,0:T(8,128)(2,1)S(1)}, u32[]{:S(2)}, u32[]{:S(2)}) %collective-permute-start.1) | collective-permute-done | bytes 262176 | tf_op jit(solution)/shard_map/ppermute | solution.py:25
  41.1 7.6 %collective-permute-done.2 = bf16[128,1024]{1,0:T(8,128)(2,1)S(1)} collective-permute-done((bf16[128,1024]{1,0:T(8,128)(2,1)S(1)}, bf16[128,1024]{1,0:T(8,128)(2,1)S(1)}, u32[]{:S(2)}, u32[]{:S(2)}) %collective-permute-start.2) | collective-permute-done | bytes 262176 | tf_op jit(solution)/shard_map/ppermute | solution.py:25
  53.8 13.3 %collective-permute-done.3 = bf16[128,1024]{1,0:T(8,128)(2,1)} collective-permute-done((bf16[128,1024]{1,0:T(8,128)(2,1)S(1)}, bf16[128,1024]{1,0:T(8,128)(2,1)}, u32[]{:S(2)}, u32[]{:S(2)}) %collective-permute-start.3) | collective-permute-done | bytes 262176 | tf_op jit(solution)/shard_map/ppermute | solution.py:25
  71.3 10.4 %all-gather.14.cloned.1.call-done = bf16[1024,1024]{1,0:T(8,128)(2,1)} async-done(((bf16[1024,128]{1,0:T(8,128)(2,1)}), bf16[1024,1024]{1,0:T(8,128)(2,1)}) %all-gather.14.cloned.1.call-update) | async-done | bytes 2097168 | tf_op jit(solution)/shard_map/all_gather | solution.py:151
  91.2 41.6 %all-gather.18.cloned.1.call-done = bf16[1024,1024]{1,0:T(8,128)(2,1)} async-done(((bf16[128,1024]{1,0:T(8,128)(2,1)}), bf16[1024,1024]{1,0:T(8,128)(2,1)}) %all-gather.18.cloned.1.call-update) | async-done | bytes 2097168 | tf_op jit(solution)/shard_map/all_gather | solution.py:196
  132.8 57.6 %all-gather.10.cloned.1.call-done = bf16[1048576]{0:T(1024)(128)(2,1)} async-done(((bf16[32768]{0:T(1024)(128)(2,1)}), bf16[1048576]{0:T(1024)(128)(2,1)}) %all-gather.10.cloned.1.call-update) | async-done | bytes 2097168 | tf_op jit(solution)/shard_map/all_gather | solution.py:145
  190.4 4.2 reshape.187
  194.5 66.6 %all-gather.8.cloned.1.call-done = bf16[3145728]{0:T(1024)(128)(2,1)} async-done(((bf16[98304]{0:T(1024)(128)(2,1)}), bf16[3145728]{0:T(1024)(128)(2,1)}) %all-gather.8.cloned.1.call-update) | async-done | bytes 6291472 | tf_op jit(solution)/shard_map/all_gather | solution.py:144
  261.1 10.5 %reshape.185 = bf16[3,1024,1024]{2,1,0:T(8,128)(2,1)} reshape(bf16[3145728]{0:T(1024)(128)(2,1)} %all-gather.8.cloned.1.call-done) | data formatting | bytes 12582912 | tf_op jit(solution)/shard_map/reshape | solution.py:147
  271.7 12.1 %convolution_bitcast_fusion = f32[3,1024,1024]{2,1,0:T(8,128)S(1)} fusion(bf16[3,1024,1024]{2,1,0:T(8,128)(2,1)} %reshape.185, bf16[1024,1024]{0,1:T(8,128)(2,1)S(1)} %copy-done.22, f32[1024]{0:T(1024)S(1)} %bitcast.189, f32[1024]{0:T(1024)S(1)} %bitcast.187, pred[1024]{0:T(1024)(128)(4,1)S(1)} %eq.17), kind=kOutput, calls=%fused_computation.100 | convolution fusion | flops 6446645248 | bytes 20980736 | tf_op jit(solution)/shard_map/td,mde->mte/dot_general | solution.py:163
  283.8 4.2 fusion.137
  288.3 5.4 copy.77
  293.7 6.7 squeeze.34
  306.1 5.5 copy.78
  311.6 6.6 squeeze.35
  327.8 4.9 copy.82
  334.3 28.1 %while.26 = (s32[]{:T(128)}, bf16[2,512,16,64]{1,3,2,0:T(8,128)(2,1)}, f32[2,16,512,1]{2,1,3,0:T(8,128)S(1)}, bf16[2,512,16,64]{1,3,2,0:T(8,128)(2,1)}, pred[2,5...) while((s32[]{:T(128)}, ...), condition=%wide.region_3.4_spmd, body=%wide.region_0.3_spmd.sunk | while | flops 1120395264 | bytes 63181432 | solution.py:172
  334.4 5.1 fusion.171
  343.3 4.9 fusion.172
  348.2 5.1 fusion.171
  357.2 4.8 fusion.172
  362.5 4.6 copy.83
  373.1 17.7 %fusion.90 = f32[1024,4096]{1,0:T(8,128)} fusion(bf16[1024,4096]{1,0:T(8,128)(2,1)} %all-gather.12.cloned.1.call-done, f32[1024,1024]{0,1:T(8,128)} %copy-done.11, f32[1024]{0:T(1024)S(1)} %bitcast.185, f32[1024]{0:T(1024)S(1)} %bitcast.176, f32[1024]{0:T(1024)S(1)} %add_rsqrt_fusion.1, f32[1024]{0:T(1024)S(1)} %broadcast_multiply_fusion.5), kind=kOutput, calls=%fused_computation.129 | convolution fusion | flops 8595177472 | bytes 29376512 | tf_op jit(solution)/shard_map/dot_general | solution.py:35
  390.8 52.6 %fusion.142 = (f32[1024]{0:T(1024)S(1)}, f32[1024,1024]{0,1:T(8,128)}) fusion(f32[1024]{0:T(1024)S(1)} %copy-done.48, bf16[4096,1024]{1,0:T(8,128)(2,1)} %all-gather.16.cloned.1.call-done, f32[1024,4096]{1,0:T(8,128)} %fusion.90, f32[4096]{0:T(1024)S(1)} %copy-done.41, f32[1024]{0:T(1024)S(1)} %bitcast.186, f32[1024]{0:T(1024)S(1)} %bitcast.177, ...), kind=kOutput, calls=%fused_computation.208 | convolution fusion | flops 8874097664 | bytes 33595392 | tf_op jit(solution)/shard_map/dot_general | solution.py:35
  448.0 21.9 %convert_reduce_fusion = (f32[4096]{0:T(1024)}, bf16[1024,4096]{1,0:T(8,128)(2,1)}) fusion(f32[1024,4096]{1,0:T(8,128)} %fusion.90, f32[4096]{0:T(1024)S(1)} %copy-done.41, bf16[4096,1024]{1,0:T(8,128)(2,1)} %all-gather.16.cloned.1.call-done, f32[1024]{0:T(1024)S(1)} %get-tuple-element.250, f32[1024]{0:T(1024)S(1)} %add_rsqrt_fusion, ...), kind=kOutput, calls=%fused_computation.71 | convolution fusion | flops 8653893632 | bytes 39899136 | tf_op jit(solution)/shard_map/dot_general | solution.py:39
  469.9 18.7 %multiply_reduce_fusion.1 = (f32[1024]{0:T(1024)}, f32[1024]{0:T(1024)S(1)}, f32[1024]{0:T(1024)S(1)}, f32[1024]{0:T(1024)}, f32[1024,1024]{0,1:T(8,128)S(1)}) fusion(f32[1024,1024]{0,1:T(8,128)} %copy-done.11, f32[1024]{0:T(1024)S(1)} %add_rsqrt_fusion.1, f32[1024]{0:T(1024)S(1)} %broadcast_multiply_fusion.5, f32[1024]{0:T(1024)S(1)} %bitcast.178, ...), kind=kOutput, calls=%fused_computation.108 | convolution fusion | flops 8608804864 | bytes 31506432 | tf_op jit(solution)/shard_map/dot_general | solution.py:39
  499.1 5.5 copy.90
  509.3 93.8 %while.27 = (s32[]{:T(128)}, bf16[2,512,16,64]{1,3,2,0:T(8,128)(2,1)}, bf16[2,512,16,64]{1,3,2,0:T(8,128)(2,1)}, bf16[2,512,16,64]{1,3,2,0:T(8,128)(2,1)}, bf16[...) while((s32[]{:T(128)}, ...), condition=%wide.region_14.15_spmd, body=%wide.region_12.14_spmd.sunk | while | flops 2724716544 | bytes 195205968 | solution.py:218
  509.3 9.6 %subtract_exponential_fusion.2 = f32[16,512,512]{1,2,0:T(8,128)} fusion(f32[16,512]{1,0:T(8,128)S(1)} %dynamic-slice_bitcast_fusion.2, pred[512]{0:T(512)(128)(4,1)S(1)} %dynamic-slice_reduce_fusion.5, bf16[2,512,16,64]{1,3,2,0:T(8,128)(2,1)} %get-tuple-element.420, s32[]{:T(128)} %get-tuple-element.403, ...), kind=kOutput, calls=%fused_computation.26.clone.1 | convolution fusion | flops 549453824 | bytes 18908672 | tf_op jit(solution)/shard_map/while/body/eval_jaxpr/qhd,khd->hqk/dot_general | solution.py:70
  518.9 10.5 %multiply_reduce_fusion.7 = (f32[16,512]{1,0:T(8,128)S(1)}, f32[16,512,512]{1,2,0:T(8,128)}) fusion(f32[16,512,512]{1,2,0:T(8,128)} %subtract_exponential_fusion.2, bf16[2,512,16,64]{1,3,2,0:T(8,128)(2,1)S(1)} %copy-done.6, s32[]{:T(128)} %get-tuple-element.403, bf16[2,512,16,64]{1,3,2,0:T(8,128)(2,1)S(1)} %copy-done.2), kind=kOutput, calls=%fused_computation.25.clone.1 | convolution fusion | flops 545251328 | bytes 35685376 | tf_op jit(solution)/shard_map/while/body/eval_jaxpr/qhd,khd->hqk/dot_general | solution.py:95
  529.4 11.9 %multiply_convert_fusion.4 = bf16[16,512,512]{1,2,0:T(8,128)(2,1)S(1)} fusion(f32[16,512,512]{1,2,0:T(8,128)} %subtract_exponential_fusion.2, f32[16,512,512]{1,2,0:T(8,128)} %get-tuple-element.366, f32[16,512]{1,0:T(8,128)S(1)} %get-tuple-element.367), kind=kLoop, calls=%fused_computation.24.clone.1 | loop fusion | flops 12582912 | bytes 41975808 | tf_op jit(solution)/shard_map/while/body/eval_jaxpr/convert_element_type | solution.py:103
  546.7 9.4 %fusion.183 = bf16[2,512,16,64]{1,3,2,0:T(8,128)(2,1)} fusion(bf16[2,512,16,64]{1,3,2,0:T(8,128)(2,1)} %get-tuple-element.406, s32[]{:T(128)} %get-tuple-element.403, f32[16,512,512]{1,2,0:T(8,128)} %subtract_exponential_fusion.2, bf16[2,512,16,64]{1,3,2,0:T(8,128)(2,1)S(1)} %copy-done.2), kind=kOutput, calls=%fused_computation.37.clone.1 | convolution fusion | flops 541589504 | bytes 18875392 | tf_op jit(solution)/shard_map/while/body/eval_jaxpr/hqk,qhd->khd/dot_general | solution.py:96
  556.2 9.6 %subtract_exponential_fusion.2 = f32[16,512,512]{1,2,0:T(8,128)} fusion(f32[16,512]{1,0:T(8,128)S(1)} %dynamic-slice_bitcast_fusion.2, pred[512]{0:T(512)(128)(4,1)S(1)} %dynamic-slice_reduce_fusion.5, bf16[2,512,16,64]{1,3,2,0:T(8,128)(2,1)} %get-tuple-element.420, s32[]{:T(128)} %get-tuple-element.403, ...), kind=kOutput, calls=%fused_computation.26.clone.1 | convolution fusion | flops 549453824 | bytes 18908672 | tf_op jit(solution)/shard_map/while/body/eval_jaxpr/qhd,khd->hqk/dot_general | solution.py:70
  565.8 10.5 %multiply_reduce_fusion.7 = (f32[16,512]{1,0:T(8,128)S(1)}, f32[16,512,512]{1,2,0:T(8,128)}) fusion(f32[16,512,512]{1,2,0:T(8,128)} %subtract_exponential_fusion.2, bf16[2,512,16,64]{1,3,2,0:T(8,128)(2,1)S(1)} %copy-done.6, s32[]{:T(128)} %get-tuple-element.403, bf16[2,512,16,64]{1,3,2,0:T(8,128)(2,1)S(1)} %copy-done.2), kind=kOutput, calls=%fused_computation.25.clone.1 | convolution fusion | flops 545251328 | bytes 35685376 | tf_op jit(solution)/shard_map/while/body/eval_jaxpr/qhd,khd->hqk/dot_general | solution.py:95
  576.3 11.9 %multiply_convert_fusion.4 = bf16[16,512,512]{1,2,0:T(8,128)(2,1)S(1)} fusion(f32[16,512,512]{1,2,0:T(8,128)} %subtract_exponential_fusion.2, f32[16,512,512]{1,2,0:T(8,128)} %get-tuple-element.366, f32[16,512]{1,0:T(8,128)S(1)} %get-tuple-element.367), kind=kLoop, calls=%fused_computation.24.clone.1 | loop fusion | flops 12582912 | bytes 41975808 | tf_op jit(solution)/shard_map/while/body/eval_jaxpr/convert_element_type | solution.py:103
  593.7 9.4 %fusion.183 = bf16[2,512,16,64]{1,3,2,0:T(8,128)(2,1)} fusion(bf16[2,512,16,64]{1,3,2,0:T(8,128)(2,1)} %get-tuple-element.406, s32[]{:T(128)} %get-tuple-element.403, f32[16,512,512]{1,2,0:T(8,128)} %subtract_exponential_fusion.2, bf16[2,512,16,64]{1,3,2,0:T(8,128)(2,1)S(1)} %copy-done.2), kind=kOutput, calls=%fused_computation.37.clone.1 | convolution fusion | flops 541589504 | bytes 18875392 | tf_op jit(solution)/shard_map/while/body/eval_jaxpr/hqk,qhd->khd/dot_general | solution.py:96
  605.0 6.2 copy.112
  613.3 6.2 copy.114
  619.6 5.5 fusion.82
  625.2 6.6 reshape.201
  631.9 4.7 copy.113
  636.6 6.5 reshape.202
  643.1 6.6 reshape.203
  649.7 12.7 %fusion.83 = bf16[1024,1024]{0,1:T(8,128)(2,1)} fusion(f32[1024,1024]{0,1:T(8,128)} %copy-done.17, bf16[3,1024,1024]{2,1,0:T(8,128)(2,1)} %reshape.185, bf16[1,1024,1024]{2,1,0:T(8,128)(2,1)} %reshape.203, bf16[1,1024,1024]{2,1,0:T(8,128)(2,1)} %reshape.202, bf16[1,1024,1024]{2,1,0:T(8,128)(2,1)S(1)} %copy-done.18), kind=kOutput, calls=%fused_computation.107 | convolution fusion | flops 6450839552 | bytes 18874368 | tf_op jit(solution)/shard_map/mte,mde->td/dot_general | solution.py:228
  662.4 4.1 copy.100
  669.2 40.5 %all-reduce = (f32[3,1024]{1,0:T(4,128)}, f32[4096]{0:T(1024)}, f32[1024]{0:T(1024)}, f32[2,1024]{1,0:T(2,128)}, f32[2,1024]{1,0:T(2,128)}) all-reduce(f32[3,1024]{1,0:T(4,128)S(1)} %pad_maximum_fusion, f32[4096]{0:T(1024)S(1)} %copy-done.42, f32[1024]{0:T(1024)S(1)} %get-tuple-element.179, ...), channel_id=1, replica_groups=mesh['dp'=8,'tensor'=4] {'dp','tensor'}, use_global_device_ids=true, to_apply=%region_18.19 | all-reduce | flops 12288 | bytes 98304 | tf_op jit(solution)/shard_map/psum | solution.py:235
  (222 shorter events, 97.6 us)
Async XLA Ops:
  7.2 74.5 %all-gather.14.cloned.1.call-start = ((), (), s32[]{:S(2)}) async-start(), calls=%async_computation.3 | async-start | bytes 2359296 | tf_op jit(solution)/shard_map/all_gather | solution.py:151
  7.9 124.8 %all-gather.18.cloned.1.call-start = ((), (), s32[]{:S(2)}) async-start(), calls=%async_computation.5 | async-start | bytes 2359296 | tf_op jit(solution)/shard_map/all_gather | solution.py:196
  8.6 181.7 %all-gather.10.cloned.1.call-start = ((), (), s32[]{:S(2)}) async-start(), calls=%async_computation.1 | async-start | bytes 2162688 | tf_op jit(solution)/shard_map/all_gather | solution.py:145
  9.4 251.7 %all-gather.8.cloned.1.call-start = ((), (), s32[]{:S(2)}) async-start(), calls=%async_computation | async-start | bytes 6488064 | tf_op jit(solution)/shard_map/all_gather | solution.py:144
  10.0 363.1 %all-gather.12.cloned.1.call-start = ((), (), s32[]{:S(2)}) async-start(), calls=%async_computation.2 | async-start | bytes 10485760 | tf_op jit(solution)/shard_map/all_gather | solution.py:154
  10.0 12.6 %collective-permute-start = (bf16[128,1024]{1,0:T(8,128)(2,1)}, bf16[128,1024]{1,0:T(8,128)(2,1)S(1)}, u32[]{:S(2)}, u32[]{:S(2)}) collective-permute-start(bf16[128,1024]{1,0:T(8,128)(2,1)} %param.24), channel_id=1, source_target_pairs={{0,4},{4,8},{8,12},{12,16},{16,20},{20,24},{24,28},{28,0},{1,5},{5... | collective-permute-start | bytes 786440 | tf_op jit(solution)/shard_map/ppermute | solution.py:25
  22.6 13.8 %collective-permute-start.1 = (bf16[128,1024]{1,0:T(8,128)(2,1)S(1)}, bf16[128,1024]{1,0:T(8,128)(2,1)S(1)}, u32[]{:S(2)}, u32[]{:S(2)}) collective-permute-start(bf16[128,1024]{1,0:T(8,128)(2,1)S(1)} %collective-permute-done), channel_id=1, source_target_pairs={{0,4},{4,8},{8,12},{12,16},{16,20},{20,24},{24,28},{28,0},{1,5},{5... | collective-permute-start | bytes 786440 | tf_op jit(solution)/shard_map/ppermute | solution.py:25
  22.6 15.2 %collective-permute-start.4 = (bf16[128,1024]{1,0:T(8,128)(2,1)}, bf16[128,1024]{1,0:T(8,128)(2,1)S(1)}, u32[]{:S(2)}, u32[]{:S(2)}) collective-permute-start(bf16[128,1024]{1,0:T(8,128)(2,1)} %param.24), channel_id=1, source_target_pairs={{4,0},{8,4},{12,8},{16,12},{20,16},{24,20},{28,24},{0,28},{5,1},{9... | collective-permute-start | bytes 786440 | tf_op jit(solution)/shard_map/ppermute | solution.py:27
  36.4 12.4 %collective-permute-start.2 = (bf16[128,1024]{1,0:T(8,128)(2,1)S(1)}, bf16[128,1024]{1,0:T(8,128)(2,1)S(1)}, u32[]{:S(2)}, u32[]{:S(2)}) collective-permute-start(bf16[128,1024]{1,0:T(8,128)(2,1)S(1)} %collective-permute-done.1), channel_id=1, source_target_pairs={{0,4},{4,8},{8,12},{12,16},{16,20},{20,24},{24,28},{28,0},{1,5},{5... | collective-permute-start | bytes 786440 | tf_op jit(solution)/shard_map/ppermute | solution.py:25
  37.8 16.0 %collective-permute-start.5 = (bf16[128,1024]{1,0:T(8,128)(2,1)S(1)}, bf16[128,1024]{1,0:T(8,128)(2,1)S(1)}, u32[]{:S(2)}, u32[]{:S(2)}) collective-permute-start(bf16[128,1024]{1,0:T(8,128)(2,1)S(1)} %collective-permute-done.4), channel_id=1, source_target_pairs={{4,0},{8,4},{12,8},{16,12},{20,16},{24,20},{28,24},{0,28},{5,1},{9... | collective-permute-start | bytes 786440 | tf_op jit(solution)/shard_map/ppermute | solution.py:27
  48.7 18.3 %collective-permute-start.3 = (bf16[128,1024]{1,0:T(8,128)(2,1)S(1)}, bf16[128,1024]{1,0:T(8,128)(2,1)}, u32[]{:S(2)}, u32[]{:S(2)}) collective-permute-start(bf16[128,1024]{1,0:T(8,128)(2,1)S(1)} %collective-permute-done.2), channel_id=1, source_target_pairs={{0,4},{4,8},{8,12},{12,16},{16,20},{20,24},{24,28},{28,0},{1,5},{5... | collective-permute-start | bytes 786440 | tf_op jit(solution)/shard_map/ppermute | solution.py:25
  53.8 15.4 %collective-permute-start.6 = (bf16[128,1024]{1,0:T(8,128)(2,1)S(1)}, bf16[128,1024]{1,0:T(8,128)(2,1)S(1)}, u32[]{:S(2)}, u32[]{:S(2)}) collective-permute-start(bf16[128,1024]{1,0:T(8,128)(2,1)S(1)} %collective-permute-done.5), channel_id=1, source_target_pairs={{4,0},{8,4},{12,8},{16,12},{20,16},{24,20},{28,24},{0,28},{5,1},{9... | collective-permute-start | bytes 786440 | tf_op jit(solution)/shard_map/ppermute | solution.py:27
  69.2 12.6 %copy-start.34 = (bf16[3,1024]{1,0:T(4,128)(2,1)S(1)}, bf16[3,1024]{1,0:T(4,128)(2,1)}, u32[]{:S(2)}) copy-start(bf16[3,1024]{1,0:T(4,128)(2,1)} %param.26) | copy-start | bytes 18436
  71.2 10.6 %copy-start.19 = (bf16[1024,1024]{1,0:T(8,128)(2,1)S(1)}, bf16[1024,1024]{1,0:T(8,128)(2,1)}, u32[]{:S(2)}) copy-start(bf16[1024,1024]{1,0:T(8,128)(2,1)} %param.18) | copy-start | bytes 6291460
  71.2 13.3 %copy-start.47 = (s32[2,512]{1,0:T(2,128)S(1)}, s32[2,512]{1,0:T(2,128)}, u32[]{:S(2)}) copy-start(s32[2,512]{1,0:T(2,128)} %param.19) | copy-start | bytes 12292
  71.2 13.5 %copy-start.46 = (bf16[4096]{0:T(1024)(128)(2,1)S(1)}, bf16[4096]{0:T(1024)(128)(2,1)}, u32[]{:S(2)}) copy-start(bf16[4096]{0:T(1024)(128)(2,1)} %param.27) | copy-start | bytes 24580
  71.2 14.1 %copy-start.51 = (bf16[1024]{0:T(1024)(128)(2,1)S(1)}, bf16[1024]{0:T(1024)(128)(2,1)}, u32[]{:S(2)}) copy-start(bf16[1024]{0:T(1024)(128)(2,1)} %param.28) | copy-start | bytes 6148
  71.2 319.6 %all-gather.16.cloned.1.call-start = ((), (), s32[]{:S(2)}) async-start(), calls=%async_computation.4 | async-start | bytes 10485760 | tf_op jit(solution)/shard_map/all_gather | solution.py:155
  81.7 388.2 %all-gather.20.cloned.1.call-start = ((), (), s32[]{:S(2)}) async-start(), calls=%async_computation.6 | async-start | bytes 10485760 | tf_op jit(solution)/shard_map/all_gather | solution.py:200
  81.8 8.0 %copy-start.52 = (s32[2]{0:T(128)S(1)}, s32[2]{0:T(128)}, u32[]{:S(2)}) copy-start(s32[2]{0:T(128)} %param.20) | copy-start | bytes 28
  81.8 8.1 %copy-start.43 = (bf16[2,1024]{1,0:T(2,128)(2,1)S(1)}, bf16[2,1024]{1,0:T(2,128)(2,1)}, u32[]{:S(2)}) copy-start(bf16[2,1024]{1,0:T(2,128)(2,1)} %param.21) | copy-start | bytes 12292
  81.8 8.1 %copy-start.44 = (bf16[2,1024]{1,0:T(2,128)(2,1)S(1)}, bf16[2,1024]{1,0:T(2,128)(2,1)}, u32[]{:S(2)}) copy-start(bf16[2,1024]{1,0:T(2,128)(2,1)} %param.29) | copy-start | bytes 12292
  81.8 8.7 %copy-start.45 = (bf16[2,1024]{1,0:T(2,128)(2,1)S(1)}, bf16[2,1024]{1,0:T(2,128)(2,1)}, u32[]{:S(2)}) copy-start(bf16[2,1024]{1,0:T(2,128)(2,1)} %param.30) | copy-start | bytes 12292
  194.5 77.1 %copy-start.22 = (bf16[1024,1024]{0,1:T(8,128)(2,1)S(1)}, bf16[1024,1024]{0,1:T(8,128)(2,1)}, u32[]{:S(2)}) copy-start(bf16[1024,1024]{0,1:T(8,128)(2,1)} %copy.75) | copy-start | bytes 6291460
  373.1 17.7 %copy-start.41 = (f32[4096]{0:T(1024)S(1)}, f32[4096]{0:T(1024)}, u32[]{:S(2)}) copy-start(f32[4096]{0:T(1024)} %convert_element_type.124) | copy-start | bytes 49156
  373.1 17.7 %copy-start.48 = (f32[1024]{0:T(1024)S(1)}, f32[1024]{0:T(1024)}, u32[]{:S(2)}) copy-start(f32[1024]{0:T(1024)} %convert_element_type.126) | copy-start | bytes 12292
  390.8 55.5 %copy-start.9 = (bf16[1024,1024]{0,1:T(8,128)(2,1)S(1)}, bf16[1024,1024]{0,1:T(8,128)(2,1)}, u32[]{:S(2)}) copy-start(bf16[1024,1024]{0,1:T(8,128)(2,1)} %copy.85) | copy-start | bytes 6291460
  443.5 26.4 %copy-start.28 = (f32[1024]{0:T(1024)}, f32[1024]{0:T(1024)S(1)}, u32[]{:S(2)}) copy-start(f32[1024]{0:T(1024)S(1)} %broadcast_multiply_fusion.4) | copy-start | bytes 12292
  446.3 23.6 %copy-start.30 = (f32[1024]{0:T(1024)}, f32[1024]{0:T(1024)S(1)}, u32[]{:S(2)}) copy-start(f32[1024]{0:T(1024)S(1)} %add_rsqrt_fusion) | copy-start | bytes 12292
  447.9 22.0 %copy-start.37 = (f32[1024]{0:T(1024)}, f32[1024]{0:T(1024)S(1)}, u32[]{:S(2)}) copy-start(f32[1024]{0:T(1024)S(1)} %get-tuple-element.250) | copy-start | bytes 12292
  448.0 21.9 %copy-start.39 = (f32[1024]{0:T(1024)}, f32[1024]{0:T(1024)S(1)}, u32[]{:S(2)}) copy-start(f32[1024]{0:T(1024)S(1)} %get-tuple-element.251) | copy-start | bytes 12292
  469.9 18.7 %copy-start.12 = (f32[1024,1024]{0,1:T(8,128)S(1)}, f32[1024,1024]{0,1:T(8,128)}, u32[]{:S(2)}) copy-start(f32[1024,1024]{0,1:T(8,128)} %copy-done.11) | copy-start | bytes 12582916
  509.3 9.6 %copy-start.2 = (bf16[2,512,16,64]{1,3,2,0:T(8,128)(2,1)S(1)}, bf16[2,512,16,64]{1,3,2,0:T(8,128)(2,1)}, u32[]{:S(2)}) copy-start(bf16[2,512,16,64]{1,3,2,0:T(8,128)(2,1)} %get-tuple-element.422) | copy-start | bytes 6291460 | tf_op jit(solution)/shard_map/while
  509.3 9.6 %copy-start.6 = (bf16[2,512,16,64]{1,3,2,0:T(8,128)(2,1)S(1)}, bf16[2,512,16,64]{1,3,2,0:T(8,128)(2,1)}, u32[]{:S(2)}) copy-start(bf16[2,512,16,64]{1,3,2,0:T(8,128)(2,1)} %get-tuple-element.423) | copy-start | bytes 6291460 | tf_op jit(solution)/shard_map/while
  529.4 11.9 %copy-start.3 = (bf16[2,512,16,64]{1,3,2,0:T(8,128)(2,1)S(1)}, bf16[2,512,16,64]{1,3,2,0:T(8,128)(2,1)}, u32[]{:S(2)}) copy-start(bf16[2,512,16,64]{1,3,2,0:T(8,128)(2,1)} %get-tuple-element.420) | copy-start | bytes 6291460 | tf_op jit(solution)/shard_map/while
  529.4 11.9 %copy-start.13 = (bf16[2,512,16,64]{1,3,2,0:T(8,128)(2,1)S(1)}, bf16[2,512,16,64]{1,3,2,0:T(8,128)(2,1)}, u32[]{:S(2)}) copy-start(bf16[2,512,16,64]{1,3,2,0:T(8,128)(2,1)} %get-tuple-element.405) | copy-start | bytes 6291460 | tf_op jit(solution)/shard_map/while
  556.2 9.6 %copy-start.2 = (bf16[2,512,16,64]{1,3,2,0:T(8,128)(2,1)S(1)}, bf16[2,512,16,64]{1,3,2,0:T(8,128)(2,1)}, u32[]{:S(2)}) copy-start(bf16[2,512,16,64]{1,3,2,0:T(8,128)(2,1)} %get-tuple-element.422) | copy-start | bytes 6291460 | tf_op jit(solution)/shard_map/while
  556.2 9.6 %copy-start.6 = (bf16[2,512,16,64]{1,3,2,0:T(8,128)(2,1)S(1)}, bf16[2,512,16,64]{1,3,2,0:T(8,128)(2,1)}, u32[]{:S(2)}) copy-start(bf16[2,512,16,64]{1,3,2,0:T(8,128)(2,1)} %get-tuple-element.423) | copy-start | bytes 6291460 | tf_op jit(solution)/shard_map/while
  576.3 11.9 %copy-start.3 = (bf16[2,512,16,64]{1,3,2,0:T(8,128)(2,1)S(1)}, bf16[2,512,16,64]{1,3,2,0:T(8,128)(2,1)}, u32[]{:S(2)}) copy-start(bf16[2,512,16,64]{1,3,2,0:T(8,128)(2,1)} %get-tuple-element.420) | copy-start | bytes 6291460 | tf_op jit(solution)/shard_map/while
  576.3 11.9 %copy-start.13 = (bf16[2,512,16,64]{1,3,2,0:T(8,128)(2,1)S(1)}, bf16[2,512,16,64]{1,3,2,0:T(8,128)(2,1)}, u32[]{:S(2)}) copy-start(bf16[2,512,16,64]{1,3,2,0:T(8,128)(2,1)} %get-tuple-element.405) | copy-start | bytes 6291460 | tf_op jit(solution)/shard_map/while
  611.2 8.4 %copy-start.10 = (bf16[1024,1024]{0,1:T(8,128)(2,1)S(1)}, bf16[1024,1024]{0,1:T(8,128)(2,1)}, u32[]{:S(2)}) copy-start(bf16[1024,1024]{0,1:T(8,128)(2,1)} %copy.85) | copy-start | bytes 6291460
  611.2 8.4 %copy-start.29 = (f32[1024]{0:T(1024)S(1)}, f32[1024]{0:T(1024)}, u32[]{:S(2)}) copy-start(f32[1024]{0:T(1024)} %copy-done.28) | copy-start | bytes 12292
  611.2 8.4 %copy-start.31 = (f32[1024]{0:T(1024)S(1)}, f32[1024]{0:T(1024)}, u32[]{:S(2)}) copy-start(f32[1024]{0:T(1024)} %copy-done.30) | copy-start | bytes 12292
  611.2 8.4 %copy-start.33 = (f32[1,1024]{1,0:T(1,128)S(1)}, f32[1,1024]{1,0:T(1,128)}, u32[]{:S(2)}) copy-start(f32[1,1024]{1,0:T(1,128)} %get-tuple-element.237) | copy-start | bytes 12292
  611.2 8.4 %copy-start.36 = (f32[1,1024]{1,0:T(1,128)S(1)}, f32[1,1024]{1,0:T(1,128)}, u32[]{:S(2)}) copy-start(f32[1,1024]{1,0:T(1,128)} %get-tuple-element.239) | copy-start | bytes 12292
  611.2 8.4 %copy-start.38 = (f32[1024]{0:T(1024)S(1)}, f32[1024]{0:T(1024)}, u32[]{:S(2)}) copy-start(f32[1024]{0:T(1024)} %copy-done.37) | copy-start | bytes 12292
  611.2 8.4 %copy-start.40 = (f32[1024]{0:T(1024)S(1)}, f32[1024]{0:T(1024)}, u32[]{:S(2)}) copy-start(f32[1024]{0:T(1024)} %copy-done.39) | copy-start | bytes 12292
  625.1 6.8 copy-start.15
  (27 other events, 111.1 us)
Sparse Core Ops, SparseCore 0:
  10.0 71.6 all-gather.13
  83.8 48.8 all-gather.17
  135.6 54.7 all-gather.9
  193.1 67.9 all-gather.7
  263.1 56.7 all-gather.11
  321.4 58.2 all-gather.15
  381.2 58.2 all-gather.19
